TPU v7x, 32 devices: a whole 2x2x4 slice. The times are simulated.
32 devices in a mesh: groups: 1, blk: 16 (over z, y, x), head: 2 (over core).
Axes of the slice: x: 2, y: 2, z: 4, core: 2. Of those that a mesh axis runs over, the one named last changes fastest.
Arguments:
- queries: bfloat16 [128, 8192], P(('groups', 'blk'), 'head'), may hold values from -6 to 6
- key_cache: bfloat16 [2, 32768, 8, 128], P('groups', 'blk', 'head'), may hold values from -18 to 18
- value_cache: bfloat16 [2, 32768, 8, 128], P('groups', 'blk', 'head'), may hold values from -6 to 6
- lengths: int32 [2], P('groups'), may hold values from 0 to 32704
- residual: bfloat16 [128, 8192], P('groups', 'blk'), may hold values from -6 to 6
- out_weight: bfloat16 [8192, 8192], P('head', 'blk'), may hold values from -0.0625 to 0.0625
- norm_gain: bfloat16 [8192], P('blk'), may hold values from 0.099609375 to 1.8984375
- gate_weight: bfloat16 [8192, 16384], P(None, ('head', 'blk')), may hold values from -0.0625 to 0.0625
- up_weight: bfloat16 [8192, 16384], P(None, ('head', 'blk')), may hold values from -0.0625 to 0.0625
- down_weight: bfloat16 [16384, 8192], P('head', 'blk'), may hold values from -0.046875 to 0.046875
Outputs:
- layer_out: bfloat16 [128, 8192], P('groups', 'blk')
Inputs may be any that keep to these rules, and one draw needn't show every extreme that they name: lengths[b] + 64 <= 32768; the cache holds sequence b's new keys and values at positions lengths[b] to lengths[b] + 63.
All inputs are finite; a program needn't handle non-finite values.
Results may differ from a plain program's by a relative error of at most 0.01.
Values may be sent and summed in bfloat16 or wider, within the bound.
No kernel may reach another device: no remote copies, remote signals or barrier semaphores. Data moves between devices by JAX's collectives and lax.ppermute only.
A program may use at most 128 MiB of HBM per device.

v0:
```python
import jax
import jax.numpy as jnp
from jax import lax
from jax.sharding import PartitionSpec as P

D = 8192
neg_big = -1e30
epsilon = 1e-06


def body(
    queries,
    key_cache,
    value_cache,
    lengths,
    residual,
    out_weight,
    norm_gain,
    gate_weight,
    up_weight,
    down_weight,
):
    blocks = lax.axis_size("blk")
    my_block = lax.axis_index("blk")
    batch, ctx_dev, kv_local, head_dim = key_cache.shape
    rows_dev = queries.shape[0]
    rows_all = rows_dev * blocks
    new_tokens = rows_all // batch
    heads_local = queries.shape[1] // head_dim
    group_size = heads_local // kv_local
    all_queries = lax.all_gather(queries, "blk", axis=0, tiled=True)
    shaped = all_queries.reshape(batch, new_tokens, kv_local, group_size, head_dim)
    scores = jnp.einsum(
        "bqkgd,bckd->bqkgc", shaped, key_cache, preferred_element_type=jnp.float32
    ) * head_dim ** (-0.5)
    query_pos = lengths[:, None] + jnp.arange(new_tokens, dtype=jnp.int32)[None, :]
    key_pos = my_block * ctx_dev + jnp.arange(ctx_dev, dtype=jnp.int32)
    visible = key_pos[None, None, None, None, :] <= query_pos[:, :, None, None, None]
    block_max = jnp.max(jnp.where(visible, scores, neg_big), axis=-1)
    weights = jnp.where(visible, jnp.exp(scores - block_max[..., None]), 0.0)
    block_sum = jnp.sum(weights, axis=-1)
    block_out = jnp.einsum(
        "bqkgc,bckd->bqkgd",
        weights.astype(jnp.bfloat16),
        value_cache,
        preferred_element_type=jnp.float32,
    )
    block_mean = (block_out / jnp.maximum(block_sum, 1.0)[..., None]).astype(jnp.bfloat16)
    row_max = block_max.reshape(rows_all, heads_local)
    row_sum = block_sum.reshape(rows_all, heads_local)
    row_mean = block_mean.reshape(rows_all, heads_local, head_dim)
    got_max, got_sum = (
        lax.all_to_all(row_max[None], "blk", split_axis=1, concat_axis=0, tiled=True),
        lax.all_to_all(row_sum[None], "blk", split_axis=1, concat_axis=0, tiled=True),
    )
    got_mean = lax.all_to_all(row_mean[None], "blk", split_axis=1, concat_axis=0, tiled=True)
    top = jnp.max(got_max, axis=0)
    factor = got_sum * jnp.exp(got_max - top[None])
    total_sum = jnp.sum(factor, axis=0)
    total_out = jnp.sum(got_mean.astype(jnp.float32) * factor[..., None], axis=0)
    attn = (
        (total_out / total_sum[..., None])
        .astype(jnp.bfloat16)
        .reshape(rows_dev, heads_local * head_dim)
    )
    proj_part = jnp.dot(
        lax.all_gather(attn, "blk", axis=0, tiled=True),
        out_weight,
        preferred_element_type=jnp.float32,
    )
    projected = lax.psum(proj_part.astype(jnp.bfloat16), "head").astype(jnp.float32)
    stream = residual.astype(jnp.float32) + projected
    squares = lax.psum(jnp.sum(stream * stream, axis=1), "blk")
    normed = (
        stream * lax.rsqrt(squares / D + epsilon)[:, None] * norm_gain.astype(jnp.float32)[None, :]
    ).astype(jnp.bfloat16)
    piece = lax.all_gather(normed, "blk", axis=1, tiled=True)
    gate = jnp.dot(piece, gate_weight, preferred_element_type=jnp.float32)
    up = jnp.dot(piece, up_weight, preferred_element_type=jnp.float32)
    hidden = (jax.nn.silu(gate) * up).astype(jnp.bfloat16)
    down_part = jnp.dot(
        lax.all_gather(hidden, "blk", axis=1, tiled=True),
        down_weight,
        preferred_element_type=jnp.float32,
    )
    down_total = lax.psum(down_part.astype(jnp.bfloat16), "head").astype(jnp.float32)
    return (stream + down_total).astype(jnp.bfloat16)


def solution(mesh):
    in_specs = (
        P(("groups", "blk"), "head"),
        P("groups", "blk", "head", None),
        P("groups", "blk", "head", None),
        P("groups"),
        P("groups", "blk"),
        P("head", "blk"),
        P("blk"),
        P(None, ("head", "blk")),
        P(None, ("head", "blk")),
        P("head", "blk"),
    )
    out_specs = P("groups", "blk")
    return jax.shard_map(body, mesh=mesh, in_specs=in_specs, out_specs=out_specs, check_vma=False)
```

profile of v0, /device:TPU:0, one launch (start us, length us, event | category | flops | bytes accessed | tf_op | source)
XLA Modules:
  0.0 444.1 jit_solution(5362369163561286765)
XLA Ops:
  6.5 0.0 all-gather.5.cloned.1.call-start
  6.5 0.7 all-gather.5.cloned.1.call-update
  7.3 0.7 iota_add_fusion.1
  8.0 0.2 broadcast_compare_fusion
  8.2 59.7 %all-gather.5.cloned.1.call-done = bf16[128,4096]{1,0:T(8,128)(2,1)} async-done(((bf16[8,4096]{1,0:T(8,128)(2,1)}), bf16[128,4096]{1,0:T(8,128)(2,1)}) %all-gather.5.cloned.1.call-update) | async-done | bytes 1048592 | tf_op jit(solution)/shard_map/all_gather | solution.py:31
  67.9 1.5 copy.45
  69.4 17.1 %fusion = (f32[2,64,4,8]{1,3,2,0:T(8,128)S(1)}, f32[2,4,2048,64,8]{2,3,4,1,0:T(8,128)}) fusion(pred[2,64,2048]{2,1,0:T(8,128)(4,1)S(1)} %broadcast_compare_fusion, bf16[2,64,4,8,128]{4,3,2,1,0:T(8,128)(2,1)S(1)} %bitcast.53, bf16[2,2048,4,128,1]{3,2,1,0,4:T(4,128)(2,1)} %bitcast.55), kind=kOutput, calls=%fused_computation.2 | convolution fusion | flops 2172645376 | bytes 39075840 | tf_op jit(solution)/shard_map/bqkgd,bckd->bqkgc/dot_general | solution.py:33
  86.5 15.1 %fusion.3 = f32[2,64,4,8]{1,3,2,0:T(8,128)S(1)} fusion(f32[2,4,2048,64,8]{2,3,4,1,0:T(8,128)} %get-tuple-element.8, f32[2,64,4,8]{1,3,2,0:T(8,128)S(1)} %get-tuple-element.7, pred[2,64,2048]{2,1,0:T(8,128)(4,1)S(1)} %broadcast_compare_fusion), kind=kLoop, calls=%fused_computation.5 | loop fusion | flops 33550336 | bytes 33849344 | tf_op jit(solution)/shard_map/reduce_sum | solution.py:41
  101.6 0.1 broadcast_in_dim_reshape.11
  101.7 0.1 copy.38
  101.8 0.5 broadcast.58
  102.3 0.8 reduce.2
  103.1 0.7 reshape.82
  103.8 4.4 %all-to-all-start.2 = ((f32[16,1,256]{2,1,0:T(1,128)}), f32[16,1,256]{2,1,0:T(1,128)S(1)}, u32[]{:S(2)}, u32[]{:S(2)}) async-start(f32[16,1,256]{2,1,0:T(1,128)} %reshape.82), calls=%async_computation.2 | async-start | bytes 32768 | tf_op jit(solution)/shard_map/all_to_all | solution.py:53
  108.3 0.1 broadcast_in_dim_reshape.10
  108.4 0.1 copy.36
  108.5 0.8 reduce
  109.3 0.7 reshape.80
  110.0 5.6 %all-to-all-done.2 = f32[16,1,256]{2,1,0:T(1,128)S(1)} async-done(((f32[16,1,256]{2,1,0:T(1,128)}), f32[16,1,256]{2,1,0:T(1,128)S(1)}, u32[]{:S(2)}, u32[]{:S(2)}) %all-to-all-start.2) | async-done | bytes 16416 | tf_op jit(solution)/shard_map/all_to_all | solution.py:53
  115.6 3.5 all-to-all-start.1
  119.1 15.6 %fusion.12 = bf16[2,64,4,8,128]{4,1,3,2,0:T(8,128)(2,1)S(1)} fusion(bf16[2,2048,4,128,1]{3,2,1,0,4:T(4,128)(2,1)} %bitcast.63, f32[2,4,2048,64,8]{2,3,4,1,0:T(8,128)} %get-tuple-element.8, f32[2,64,4,8]{1,3,2,0:T(8,128)S(1)} %get-tuple-element.7, pred[2,64,2048]{2,1,0:T(8,128)(4,1)S(1)} %broadcast_compare_fusion, f32[2,64,4,8]{1,3,2,0:T(8,128)S(1)} %broadcast_maximum_fusion), kind=kOutput, calls=%fused_computation.15 | convolution fusion | flops 2182086656 | bytes 39092224 | tf_op jit(solution)/shard_map/bqkgc,bckd->bqkgd/dot_general | solution.py:42
  134.7 0.0 copy-start.3
  134.7 0.0 copy-start.1
  134.8 1.7 copy.33
  136.4 0.0 all-to-all-done.1
  136.4 6.9 %all-to-all-start = ((bf16[1,128,32,128]{3,2,0,1:T(8,128)(2,1)}), bf16[1,128,32,128]{3,2,0,1:T(8,128)(2,1)S(1)}, u32[]{:S(2)}, u32[]{:S(2)}) async-start(bf16[1,128,32,128]{3,2,0,1:T(8,128)(2,1)} %bitcast.5), calls=%async_computation | async-start | bytes 2097152 | tf_op jit(solution)/shard_map/all_to_all | solution.py:56
  143.3 0.2 all-gather.7.cloned.1.call-start
  143.5 0.6 reduce.3
  144.2 0.1 reshape.83
  144.3 0.6 reduce.1
  145.0 0.1 reshape.81
  145.2 19.7 %all-to-all-done = bf16[1,128,32,128]{3,2,0,1:T(8,128)(2,1)S(1)} async-done(((bf16[1,128,32,128]{3,2,0,1:T(8,128)(2,1)}), bf16[1,128,32,128]{3,2,0,1:T(8,128)(2,1)S(1)}, u32[]{:S(2)}, u32[]{:S(2)}) %all-to-all-start) | async-done | bytes 1048608 | tf_op jit(solution)/shard_map/all_to_all | solution.py:56
  164.9 0.7 fusion.11
  165.6 0.1 fusion.19
  165.8 0.7 copy.60
  166.4 0.0 all-gather.7.cloned.1.call-update
  166.4 0.0 all-reduce.3.cloned.1.call-start
  166.5 54.4 %all-gather.7.cloned.1.call-done = bf16[128,4096]{1,0:T(8,128)(2,1)} async-done(((bf16[8,4096]{1,0:T(8,128)(2,1)}), bf16[128,4096]{1,0:T(8,128)(2,1)}) %all-gather.7.cloned.1.call-update) | async-done | bytes 1048592 | tf_op jit(solution)/shard_map/all_gather | solution.py:67
  220.9 3.9 convolution_convert_fusion
  224.8 0.0 all-reduce.3.cloned.1.call-update
  224.8 0.0 all-gather.9.cloned.1.call-start
  224.8 0.0 copy-done.3
  224.9 16.8 %all-reduce.3.cloned.1.call-done = bf16[128,512]{1,0:T(8,128)(2,1)} async-done(((bf16[128,512]{1,0:T(8,128)(2,1)}), bf16[128,512]{1,0:T(8,128)(2,1)}) %all-reduce.3.cloned.1.call-update) | async-done | bytes 131088 | tf_op jit(solution)/shard_map/psum | solution.py:71
  241.7 0.0 copy-done.1
  241.7 1.0 multiply_reduce_fusion
  242.7 42.0 %psum.22 = f32[128]{0:T(128)S(1)} all-reduce(f32[128]{0:T(128)S(1)} %multiply_reduce_fusion), channel_id=1, replica_groups=mesh['groups'=1,'blk'=16,'head'=2] {'blk'}, use_global_device_ids=true, to_apply=%region_7.8 | all-reduce | flops 128 | bytes 1024 | tf_op jit(solution)/shard_map/psum | solution.py:73
  284.7 1.7 multiply_convert_fusion
  286.4 0.0 all-gather.9.cloned.1.call-update
  286.4 0.0 all-gather.11.cloned.1.call-start
  286.5 56.9 %all-gather.9.cloned.1.call-done = bf16[128,8192]{1,0:T(8,128)(2,1)} async-done(((bf16[128,512]{1,0:T(8,128)(2,1)}), bf16[128,8192]{1,0:T(8,128)(2,1)}) %all-gather.9.cloned.1.call-update) | async-done | bytes 2097168 | tf_op jit(solution)/shard_map/all_gather | solution.py:77
  343.3 0.0 copy-start
  343.3 5.4 %fusion.23 = f32[128,512]{1,0:T(8,128)S(1)} fusion(bf16[128,8192]{1,0:T(8,128)(2,1)} %all-gather.9.cloned.1.call-done, bf16[8192,512]{1,0:T(8,128)(2,1)} %param.17), kind=kOutput, calls=%fused_computation.37 | convolution fusion | flops 1073741824 | bytes 10747904 | tf_op jit(solution)/shard_map/dot_general | solution.py:78
  348.7 0.0 copy-done
  348.7 5.4 %fusion.17 = bf16[128,512]{1,0:T(8,128)(2,1)} fusion(bf16[128,8192]{1,0:T(8,128)(2,1)S(1)} %copy-done, bf16[8192,512]{1,0:T(8,128)(2,1)} %param.18, f32[128,512]{1,0:T(8,128)S(1)} %fusion.23), kind=kOutput, calls=%fused_computation.17 | convolution fusion | flops 1074135040 | bytes 10878976 | tf_op jit(solution)/shard_map/dot_general | solution.py:79
  354.2 0.0 all-gather.11.cloned.1.call-update
  354.2 0.0 copy-start.2
  354.2 0.0 all-reduce.5.cloned.1.call-start
  354.3 59.2 %all-gather.11.cloned.1.call-done = bf16[128,8192]{1,0:T(8,128)(2,1)} async-done(((bf16[128,512]{1,0:T(8,128)(2,1)}), bf16[128,8192]{1,0:T(8,128)(2,1)}) %all-gather.11.cloned.1.call-update) | async-done | bytes 2097168 | tf_op jit(solution)/shard_map/all_gather | solution.py:82
  413.4 5.9 %convolution_convert_fusion.1 = bf16[128,512]{1,0:T(8,128)(2,1)} fusion(bf16[128,8192]{1,0:T(8,128)(2,1)} %all-gather.11.cloned.1.call-done, bf16[8192,512]{1,0:T(8,128)(2,1)} %param.19), kind=kOutput, calls=%fused_computation.19 | convolution fusion | flops 1073807360 | bytes 10616832 | tf_op jit(solution)/shard_map/dot_general | solution.py:81
  419.4 0.0 all-reduce.5.cloned.1.call-update
  419.4 16.2 %all-reduce.5.cloned.1.call-done = bf16[128,512]{1,0:T(8,128)(2,1)} async-done(((bf16[128,512]{1,0:T(8,128)(2,1)}), bf16[128,512]{1,0:T(8,128)(2,1)}) %all-reduce.5.cloned.1.call-update) | async-done | bytes 131088 | tf_op jit(solution)/shard_map/psum | solution.py:86
  435.6 0.0 copy-done.2
  435.6 1.6 add_convert_fusion
  (8 shorter events, 0.1 us)
Async XLA Ops:
  6.5 61.4 %all-gather.5.cloned.1.call-start = ((), (), s32[]{:S(2)}) async-start(), calls=%async_computation.3 | async-start | bytes 1114112 | tf_op jit(solution)/shard_map/all_gather | solution.py:31
  103.8 11.8 %all-to-all-start.2 = ((f32[16,1,256]{2,1,0:T(1,128)}), f32[16,1,256]{2,1,0:T(1,128)S(1)}, u32[]{:S(2)}, u32[]{:S(2)}) async-start(f32[16,1,256]{2,1,0:T(1,128)} %reshape.82), calls=%async_computation.2 | async-start | bytes 32768 | tf_op jit(solution)/shard_map/all_to_all | solution.py:53
  115.6 20.8 %all-to-all-start.1 = ((f32[16,1,256]{2,1,0:T(1,128)}), f32[16,1,256]{2,1,0:T(1,128)S(1)}, u32[]{:S(2)}, u32[]{:S(2)}) async-start(f32[16,1,256]{2,1,0:T(1,128)} %reshape.80), calls=%async_computation.1 | async-start | bytes 32768 | tf_op jit(solution)/shard_map/all_to_all | solution.py:54
  134.7 90.1 %copy-start.3 = (bf16[512]{0:T(512)(128)(2,1)S(1)}, bf16[512]{0:T(512)(128)(2,1)}, u32[]{:S(2)}) copy-start(bf16[512]{0:T(512)(128)(2,1)} %param.16) | copy-start | bytes 3076
  134.7 106.9 %copy-start.1 = (bf16[128,512]{1,0:T(8,128)(2,1)S(1)}, bf16[128,512]{1,0:T(8,128)(2,1)}, u32[]{:S(2)}) copy-start(bf16[128,512]{1,0:T(8,128)(2,1)} %param.14) | copy-start | bytes 393220
  136.4 28.5 %all-to-all-start = ((bf16[1,128,32,128]{3,2,0,1:T(8,128)(2,1)}), bf16[1,128,32,128]{3,2,0,1:T(8,128)(2,1)S(1)}, u32[]{:S(2)}, u32[]{:S(2)}) async-start(bf16[1,128,32,128]{3,2,0,1:T(8,128)(2,1)} %bitcast.5), calls=%async_computation | async-start | bytes 2097152 | tf_op jit(solution)/shard_map/all_to_all | solution.py:56
  143.3 77.6 %all-gather.7.cloned.1.call-start = ((), (), s32[]{:S(2)}) async-start(), calls=%async_computation.4 | async-start | bytes 1114112 | tf_op jit(solution)/shard_map/all_gather | solution.py:67
  166.4 75.2 %all-reduce.3.cloned.1.call-start = ((), (), s32[]{:S(2)}) async-start(), calls=%async_computation.5 | async-start | bytes 262144 | tf_op jit(solution)/shard_map/psum | solution.py:71
  224.8 118.5 %all-gather.9.cloned.1.call-start = ((), (), s32[]{:S(2)}) async-start(), calls=%async_computation.6 | async-start | bytes 2228224 | tf_op jit(solution)/shard_map/all_gather | solution.py:77
  286.4 127.0 %all-gather.11.cloned.1.call-start = ((), (), s32[]{:S(2)}) async-start(), calls=%async_computation.7 | async-start | bytes 2228224 | tf_op jit(solution)/shard_map/all_gather | solution.py:82
  343.3 5.4 %copy-start = (bf16[128,8192]{1,0:T(8,128)(2,1)S(1)}, bf16[128,8192]{1,0:T(8,128)(2,1)}, u32[]{:S(2)}) copy-start(bf16[128,8192]{1,0:T(8,128)(2,1)} %all-gather.9.cloned.1.call-done) | copy-start | bytes 6291460
  354.2 81.4 %copy-start.2 = (bf16[128,512]{1,0:T(8,128)(2,1)S(1)}, bf16[128,512]{1,0:T(8,128)(2,1)}, u32[]{:S(2)}) copy-start(bf16[128,512]{1,0:T(8,128)(2,1)} %all-reduce.3.cloned.1.call-done) | copy-start | bytes 393220
  354.2 81.4 %all-reduce.5.cloned.1.call-start = ((), (), s32[]{:S(2)}) async-start(), calls=%async_computation.8 | async-start | bytes 262144 | tf_op jit(solution)/shard_map/psum | solution.py:86
Sparse Core Ops, SparseCore 0:
  10.1 57.7 all-gather.4
  166.6 54.2 all-gather.6
  224.9 16.7 all-reduce.2
  286.5 56.7 all-gather.8
  354.3 59.0 all-gather.10
  419.5 16.0 all-reduce.4
where the time goes:
time: 445 us; the launch traced here: 444 us
  waiting for transfers between devices  289 us (65%)
  matrix products  53.4 us (12%)
  blocking collectives  42 us (9%)
  other arithmetic  24 us (5%)
  starting transfers between devices  15.2 us (3%)
  between operations  13.7 us (3%)
  local copies, waits for them, and re-layouts  6.46 us (1%)
    all_gather x1, waiting for transfers between devices, body(): all_queries = lax.all_gather(queries, 'blk', axis=0, tiled=True)  59.7 us
    all_gather x1, waiting for transfers between devices, body(): lax.all_gather(hidden, 'blk', axis=1, tiled=True)  59.2 us
    all_gather x1, waiting for transfers between devices, body(): piece = lax.all_gather(normed, 'blk', axis=1, tiled=True)  56.9 us
    all_gather x1, waiting for transfers between devices, body(): lax.all_gather(attn, 'blk', axis=0, tiled=True)  54.4 us
    psum x1, blocking collectives, body(): squares = lax.psum(jnp.sum(stream * stream, axis=1), 'blk')  42 us
    all_to_all x1, waiting for transfers between devices, body(): lax.all_to_all(row_mean[None], 'blk', split_axis=1, concat_axis=0, tiled=...  19.7 us
    dot_general x1, matrix products, body(): jnp.einsum('bqkgd,bckd->bqkgc', shaped, key_cache, preferred_element_type...  17.1 us
    psum x1, waiting for transfers between devices, body(): lax.psum(proj_part.astype(jnp.bfloat16), 'head').astype(jnp.float32)  16.8 us
  transfers between devices with their start and end apart: 9, of which 8 were waited for; matrix products, arithmetic and copies ran while one was open for 5% of the time, Pallas kernels for 0%

commit v1 on v0

--- a/solution.py
+++ b/solution.py
@@ -1,3 +1,4 @@
+import functools
 import jax
 import jax.numpy as jnp
 from jax import lax
@@ -6,6 +7,36 @@
 D = 8192
 neg_big = -1e30
 epsilon = 1e-06
+
+
+def do_yards(here_x, on_dim):
+    here_x = jnp.moveaxis(here_x, 0, on_dim)
+    w1 = here_x.shape
+    return here_x.reshape(*w1[:on_dim], w1[on_dim] * w1[on_dim + 1], *w1[on_dim + 2 :])
+
+
+def _group_plane(arr, shard_axis):
+    shares = lax.axis_size(shard_axis)
+    z = arr[None]
+    for tick in range(shares.bit_length() - 1):
+        y = 1 << tick
+        queue = []
+        hop_no = 0
+        while hop_no < shares:
+            queue.append((hop_no, hop_no ^ y))
+            hop_no = hop_no + 1
+        q_next = lax.ppermute(z, axis_name=shard_axis, perm=queue)
+        part_now = jnp.stack([z, q_next])
+        h_now = lax.axis_index(shard_axis) >> tick & 1
+        z = jnp.where(h_now == 0, part_now, part_now[::-1]).reshape(-1, *arr.shape)
+    return z
+
+
+def expand_cells_in(point, vals, which_dim):
+    return do_yards(_group_plane(point, vals), which_dim)
+
+
+place_meshes_on_mesh = functools.partial(expand_cells_in, vals="blk", which_dim=0)
 
 
 def body(
@@ -63,11 +94,7 @@
         .astype(jnp.bfloat16)
         .reshape(rows_dev, heads_local * head_dim)
     )
-    proj_part = jnp.dot(
-        lax.all_gather(attn, "blk", axis=0, tiled=True),
-        out_weight,
-        preferred_element_type=jnp.float32,
-    )
+    proj_part = jnp.dot(place_meshes_on_mesh(attn), out_weight, preferred_element_type=jnp.float32)
     projected = lax.psum(proj_part.astype(jnp.bfloat16), "head").astype(jnp.float32)
     stream = residual.astype(jnp.float32) + projected
     squares = lax.psum(jnp.sum(stream * stream, axis=1), "blk")

time: 445 us -> 426 us (0.957)
  waiting for transfers between devices: 289 us -> 266 us
  starting transfers between devices: 15.2 us -> 19.7 us
    all_gather x1 -> x0, waiting for transfers between devices: 54.4 us -> none  [body(): lax.all_gather(attn, 'blk', axis=0, tiled=True)]
    ppermute x0 -> x4, waiting for transfers between devices: none -> 31.3 us  [_group_plane(): q_next = lax.ppermute(z, axis_name=shard_axis, perm=queue)]
    ppermute x0 -> x4, starting transfers between devices: none -> 4.54 us  [_group_plane(): q_next = lax.ppermute(z, axis_name=shard_axis, perm=queue)]
  transfers between devices with their start and end apart: 9 -> 12, of which waited for: 8 -> 11; matrix products, arithmetic and copies ran while one was open for 5% -> 5% of each run, Pallas kernels for 0% -> 0%
where the time goes in v1:
time: 426 us; the launch traced here: 425 us
  waiting for transfers between devices  266 us (62%)
  matrix products  53.1 us (12%)
  blocking collectives  42 us (10%)
  other arithmetic  24.6 us (6%)
  starting transfers between devices  19.7 us (5%)
  between operations  13.4 us (3%)
  local copies, waits for them, and re-layouts  5.87 us (1%)
    all_gather x1, waiting for transfers between devices, body(): all_queries = lax.all_gather(queries, 'blk', axis=0, tiled=True)  59.7 us
    all_gather x1, waiting for transfers between devices, body(): lax.all_gather(hidden, 'blk', axis=1, tiled=True)  59.2 us
    all_gather x1, waiting for transfers between devices, body(): piece = lax.all_gather(normed, 'blk', axis=1, tiled=True)  56.9 us
    psum x1, blocking collectives, body(): squares = lax.psum(jnp.sum(stream * stream, axis=1), 'blk')  42 us
    ppermute x4, waiting for transfers between devices, _group_plane(): q_next = lax.ppermute(z, axis_name=shard_axis, perm=queue)  31.3 us
    all_to_all x1, waiting for transfers between devices, body(): lax.all_to_all(row_mean[None], 'blk', split_axis=1, concat_axis=0, tiled=...  19.7 us
    psum x1, waiting for transfers between devices, body(): lax.psum(proj_part.astype(jnp.bfloat16), 'head').astype(jnp.float32)  17.1 us
    dot_general x1, matrix products, body(): jnp.einsum('bqkgd,bckd->bqkgc', shaped, key_cache, preferred_element_type...  17.1 us
  transfers between devices with their start and end apart: 12, of which 11 were waited for; matrix products, arithmetic and copies ran while one was open for 5% of the time, Pallas kernels for 0%

profile of v1, /device:TPU:0, one launch (start us, length us, event | category | flops | bytes accessed | tf_op | source)
XLA Modules:
  0.0 425.1 jit_solution(14439871669304791414)
XLA Ops:
  6.5 0.7 all-gather.4.cloned.1.call-update
  7.3 0.7 iota_add_fusion.1
  8.0 0.2 broadcast_compare_fusion
  8.2 59.7 %all-gather.4.cloned.1.call-done = bf16[128,4096]{1,0:T(8,128)(2,1)} async-done(((bf16[8,4096]{1,0:T(8,128)(2,1)}), bf16[128,4096]{1,0:T(8,128)(2,1)}) %all-gather.4.cloned.1.call-update) | async-done | bytes 1048592 | tf_op jit(solution)/shard_map/all_gather | solution.py:62
  67.9 1.5 copy.45
  69.4 17.1 %fusion = (f32[2,64,4,8]{1,3,2,0:T(8,128)S(1)}, f32[2,4,2048,64,8]{2,3,4,1,0:T(8,128)}) fusion(pred[2,64,2048]{2,1,0:T(8,128)(4,1)S(1)} %broadcast_compare_fusion, bf16[2,64,4,8,128]{4,3,2,1,0:T(8,128)(2,1)S(1)} %bitcast.61, bf16[2,2048,4,128,1]{3,2,1,0,4:T(4,128)(2,1)} %bitcast.64), kind=kOutput, calls=%fused_computation.2 | convolution fusion | flops 2172645376 | bytes 39075840 | tf_op jit(solution)/shard_map/bqkgd,bckd->bqkgc/dot_general | solution.py:64
  86.5 15.1 %fusion.3 = f32[2,64,4,8]{1,3,2,0:T(8,128)S(1)} fusion(f32[2,4,2048,64,8]{2,3,4,1,0:T(8,128)} %get-tuple-element.10, f32[2,64,4,8]{1,3,2,0:T(8,128)S(1)} %get-tuple-element.9, pred[2,64,2048]{2,1,0:T(8,128)(4,1)S(1)} %broadcast_compare_fusion), kind=kLoop, calls=%fused_computation.5 | loop fusion | flops 33550336 | bytes 33849344 | tf_op jit(solution)/shard_map/reduce_sum | solution.py:72
  101.6 0.1 broadcast_in_dim_reshape.12
  101.7 0.1 copy.38
  101.8 0.5 broadcast.61
  102.3 0.8 reduce.2
  103.1 0.7 reshape.137
  103.8 4.4 %all-to-all-start.2 = ((f32[16,1,256]{2,1,0:T(1,128)}), f32[16,1,256]{2,1,0:T(1,128)S(1)}, u32[]{:S(2)}, u32[]{:S(2)}) async-start(f32[16,1,256]{2,1,0:T(1,128)} %reshape.137), calls=%async_computation.2 | async-start | bytes 32768 | tf_op jit(solution)/shard_map/all_to_all | solution.py:84
  108.3 0.1 broadcast_in_dim_reshape.11
  108.4 0.1 copy.36
  108.5 0.8 reduce
  109.3 0.7 reshape.135
  110.0 5.6 %all-to-all-done.2 = f32[16,1,256]{2,1,0:T(1,128)S(1)} async-done(((f32[16,1,256]{2,1,0:T(1,128)}), f32[16,1,256]{2,1,0:T(1,128)S(1)}, u32[]{:S(2)}, u32[]{:S(2)}) %all-to-all-start.2) | async-done | bytes 16416 | tf_op jit(solution)/shard_map/all_to_all | solution.py:84
  115.6 3.5 all-to-all-start.1
  119.1 15.6 %fusion.12 = bf16[2,64,4,8,128]{4,1,3,2,0:T(8,128)(2,1)S(1)} fusion(bf16[2,2048,4,128,1]{3,2,1,0,4:T(4,128)(2,1)} %bitcast.79, f32[2,4,2048,64,8]{2,3,4,1,0:T(8,128)} %get-tuple-element.10, f32[2,64,4,8]{1,3,2,0:T(8,128)S(1)} %get-tuple-element.9, pred[2,64,2048]{2,1,0:T(8,128)(4,1)S(1)} %broadcast_compare_fusion, f32[2,64,4,8]{1,3,2,0:T(8,128)S(1)} %broadcast_maximum_fusion), kind=kOutput, calls=%fused_computation.15 | convolution fusion | flops 2182086656 | bytes 39092224 | tf_op jit(solution)/shard_map/bqkgc,bckd->bqkgd/dot_general | solution.py:73
  134.7 1.7 copy.33
  136.4 0.0 all-to-all-done.1
  136.4 6.9 %all-to-all-start = ((bf16[1,128,32,128]{3,2,0,1:T(8,128)(2,1)}), bf16[1,128,32,128]{3,2,0,1:T(8,128)(2,1)S(1)}, u32[]{:S(2)}, u32[]{:S(2)}) async-start(bf16[1,128,32,128]{3,2,0,1:T(8,128)(2,1)} %bitcast.5), calls=%async_computation | async-start | bytes 2097152 | tf_op jit(solution)/shard_map/all_to_all | solution.py:87
  143.3 0.0 copy-start.3
  143.3 0.0 copy-start.1
  143.3 0.2 all-reduce.3.cloned.1.call-start
  143.5 0.6 reduce.3
  144.2 0.1 reshape.138
  144.3 0.6 reduce.1
  145.0 0.1 reshape.136
  145.2 19.7 %all-to-all-done = bf16[1,128,32,128]{3,2,0,1:T(8,128)(2,1)S(1)} async-done(((bf16[1,128,32,128]{3,2,0,1:T(8,128)(2,1)}), bf16[1,128,32,128]{3,2,0,1:T(8,128)(2,1)S(1)}, u32[]{:S(2)}, u32[]{:S(2)}) %all-to-all-start) | async-done | bytes 1048608 | tf_op jit(solution)/shard_map/all_to_all | solution.py:87
  164.9 0.7 fusion.11
  165.6 0.1 divide_convert_fusion
  165.8 0.6 collective-permute-start
  166.4 3.7 collective-permute-done
  170.2 1.4 collective-permute-start.1
  171.5 3.6 collective-permute-done.1
  175.3 2.0 collective-permute-start.2
  177.3 7.9 %collective-permute-done.2 = bf16[4,8,4096]{2,1,0:T(8,128)(2,1)S(1)} collective-permute-done((bf16[4,8,4096]{2,1,0:T(8,128)(2,1)S(1)}, bf16[4,8,4096]{2,1,0:T(8,128)(2,1)S(1)}, u32[]{:S(2)}, u32[]{:S(2)}) %collective-permute-start.2) | collective-permute-done | bytes 262176 | tf_op jit(solution)/shard_map/ppermute | solution.py:28
  185.2 0.1 pad_maximum_fusion.1
  185.3 0.1 reverse_select_fusion.1
  185.4 0.5 collective-permute-start.3
  185.9 16.1 %collective-permute-done.3 = bf16[8,8,4096]{2,1,0:T(8,128)(2,1)S(1)} collective-permute-done((bf16[8,8,4096]{2,1,0:T(8,128)(2,1)S(1)}, bf16[8,8,4096]{2,1,0:T(8,128)(2,1)S(1)}, u32[]{:S(2)}, u32[]{:S(2)}) %collective-permute-start.3) | collective-permute-done | bytes 524320 | tf_op jit(solution)/shard_map/ppermute | solution.py:28
  201.9 0.1 pad_maximum_fusion
  202.0 0.2 reverse_select_fusion
  202.2 3.6 convolution_convert_fusion
  205.8 0.0 all-reduce.3.cloned.1.call-update
  205.9 0.0 all-gather.6.cloned.1.call-start
  205.9 17.1 %all-reduce.3.cloned.1.call-done = bf16[128,512]{1,0:T(8,128)(2,1)} async-done(((bf16[128,512]{1,0:T(8,128)(2,1)}), bf16[128,512]{1,0:T(8,128)(2,1)}) %all-reduce.3.cloned.1.call-update) | async-done | bytes 131088 | tf_op jit(solution)/shard_map/psum | solution.py:98
  223.0 1.0 multiply_reduce_fusion
  224.1 42.0 %psum.22 = f32[128]{0:T(128)S(1)} all-reduce(f32[128]{0:T(128)S(1)} %multiply_reduce_fusion), channel_id=1, replica_groups=mesh['groups'=1,'blk'=16,'head'=2] {'blk'}, use_global_device_ids=true, to_apply=%region_7.8 | all-reduce | flops 128 | bytes 1024 | tf_op jit(solution)/shard_map/psum | solution.py:100
  266.1 1.7 multiply_convert_fusion
  267.7 0.0 all-gather.6.cloned.1.call-update
  267.8 0.0 all-gather.8.cloned.1.call-start
  267.8 56.9 %all-gather.6.cloned.1.call-done = bf16[128,8192]{1,0:T(8,128)(2,1)} async-done(((bf16[128,512]{1,0:T(8,128)(2,1)}), bf16[128,8192]{1,0:T(8,128)(2,1)}) %all-gather.6.cloned.1.call-update) | async-done | bytes 2097168 | tf_op jit(solution)/shard_map/all_gather | solution.py:104
  324.7 5.4 %fusion.24 = f32[128,512]{1,0:T(8,128)S(1)} fusion(bf16[128,8192]{1,0:T(8,128)(2,1)} %all-gather.6.cloned.1.call-done, bf16[8192,512]{1,0:T(8,128)(2,1)} %param.17), kind=kOutput, calls=%fused_computation.45 | convolution fusion | flops 1073741824 | bytes 10747904 | tf_op jit(solution)/shard_map/dot_general | solution.py:105
  330.1 5.4 %fusion.17 = bf16[128,512]{1,0:T(8,128)(2,1)} fusion(bf16[128,8192]{1,0:T(8,128)(2,1)S(1)} %copy-done, bf16[8192,512]{1,0:T(8,128)(2,1)} %param.18, f32[128,512]{1,0:T(8,128)S(1)} %fusion.24), kind=kOutput, calls=%fused_computation.18 | convolution fusion | flops 1074135040 | bytes 10878976 | tf_op jit(solution)/shard_map/dot_general | solution.py:106
  335.5 0.0 all-gather.8.cloned.1.call-update
  335.6 0.0 all-reduce.5.cloned.1.call-start
  335.6 59.2 %all-gather.8.cloned.1.call-done = bf16[128,8192]{1,0:T(8,128)(2,1)} async-done(((bf16[128,512]{1,0:T(8,128)(2,1)}), bf16[128,8192]{1,0:T(8,128)(2,1)}) %all-gather.8.cloned.1.call-update) | async-done | bytes 2097168 | tf_op jit(solution)/shard_map/all_gather | solution.py:109
  394.8 5.9 %convolution_convert_fusion.1 = bf16[128,512]{1,0:T(8,128)(2,1)} fusion(bf16[128,8192]{1,0:T(8,128)(2,1)} %all-gather.8.cloned.1.call-done, bf16[8192,512]{1,0:T(8,128)(2,1)} %param.19), kind=kOutput, calls=%fused_computation.20 | convolution fusion | flops 1073807360 | bytes 10616832 | tf_op jit(solution)/shard_map/dot_general | solution.py:108
  400.7 0.0 all-reduce.5.cloned.1.call-update
  400.7 16.2 %all-reduce.5.cloned.1.call-done = bf16[128,512]{1,0:T(8,128)(2,1)} async-done(((bf16[128,512]{1,0:T(8,128)(2,1)}), bf16[128,512]{1,0:T(8,128)(2,1)}) %all-reduce.5.cloned.1.call-update) | async-done | bytes 131088 | tf_op jit(solution)/shard_map/psum | solution.py:113
  417.0 1.6 add_convert_fusion
  (21 shorter events, 0.3 us)
Async XLA Ops:
  6.5 61.4 %all-gather.4.cloned.1.call-start = ((), (), s32[]{:S(2)}) async-start(), calls=%async_computation.3 | async-start | bytes 1114112 | tf_op jit(solution)/shard_map/all_gather | solution.py:62
  103.8 11.8 %all-to-all-start.2 = ((f32[16,1,256]{2,1,0:T(1,128)}), f32[16,1,256]{2,1,0:T(1,128)S(1)}, u32[]{:S(2)}, u32[]{:S(2)}) async-start(f32[16,1,256]{2,1,0:T(1,128)} %reshape.137), calls=%async_computation.2 | async-start | bytes 32768 | tf_op jit(solution)/shard_map/all_to_all | solution.py:84
  115.6 20.8 %all-to-all-start.1 = ((f32[16,1,256]{2,1,0:T(1,128)}), f32[16,1,256]{2,1,0:T(1,128)S(1)}, u32[]{:S(2)}, u32[]{:S(2)}) async-start(f32[16,1,256]{2,1,0:T(1,128)} %reshape.135), calls=%async_computation.1 | async-start | bytes 32768 | tf_op jit(solution)/shard_map/all_to_all | solution.py:85
  136.4 28.5 %all-to-all-start = ((bf16[1,128,32,128]{3,2,0,1:T(8,128)(2,1)}), bf16[1,128,32,128]{3,2,0,1:T(8,128)(2,1)S(1)}, u32[]{:S(2)}, u32[]{:S(2)}) async-start(bf16[1,128,32,128]{3,2,0,1:T(8,128)(2,1)} %bitcast.5), calls=%async_computation | async-start | bytes 2097152 | tf_op jit(solution)/shard_map/all_to_all | solution.py:87
  143.3 62.6 %copy-start.3 = (bf16[512]{0:T(512)(128)(2,1)S(1)}, bf16[512]{0:T(512)(128)(2,1)}, u32[]{:S(2)}) copy-start(bf16[512]{0:T(512)(128)(2,1)} %param.16) | copy-start | bytes 3076
  143.3 79.7 %copy-start.1 = (bf16[128,512]{1,0:T(8,128)(2,1)S(1)}, bf16[128,512]{1,0:T(8,128)(2,1)}, u32[]{:S(2)}) copy-start(bf16[128,512]{1,0:T(8,128)(2,1)} %param.14) | copy-start | bytes 393220
  143.3 79.7 %all-reduce.3.cloned.1.call-start = ((), (), s32[]{:S(2)}) async-start(), calls=%async_computation.4 | async-start | bytes 262144 | tf_op jit(solution)/shard_map/psum | solution.py:98
  165.8 4.3 %collective-permute-start = (bf16[1,8,4096]{2,1,0:T(8,128)(2,1)S(1)}, bf16[1,8,4096]{2,1,0:T(8,128)(2,1)S(1)}, u32[]{:S(2)}, u32[]{:S(2)}) collective-permute-start(bf16[1,8,4096]{2,1,0:T(8,128)(2,1)S(1)} %convert_element_type.72), channel_id=1, source_target_pairs={{0,2},{2,0},{4,6},{6,4},{8,10},{10,8},{12,14},{14,12},{16,18},{18,... | collective-permute-start | bytes 196616 | tf_op jit(solution)/shard_map/ppermute | solution.py:28
  170.2 5.0 %collective-permute-start.1 = (bf16[2,8,4096]{2,1,0:T(8,128)(2,1)S(1)}, bf16[2,8,4096]{2,1,0:T(8,128)(2,1)S(1)}, u32[]{:S(2)}, u32[]{:S(2)}) collective-permute-start(bf16[2,8,4096]{2,1,0:T(8,128)(2,1)S(1)} %get-tuple-element.8), channel_id=1, source_target_pairs={{0,4},{2,6},{4,0},{6,2},{8,12},{10,14},{12,8},{14,10},{16,20},{18,... | collective-permute-start | bytes 393224 | tf_op jit(solution)/shard_map/ppermute | solution.py:28
  175.3 9.9 %collective-permute-start.2 = (bf16[4,8,4096]{2,1,0:T(8,128)(2,1)S(1)}, bf16[4,8,4096]{2,1,0:T(8,128)(2,1)S(1)}, u32[]{:S(2)}, u32[]{:S(2)}) collective-permute-start(bf16[4,8,4096]{2,1,0:T(8,128)(2,1)S(1)} %bitcast.68), channel_id=1, source_target_pairs={{0,8},{2,10},{4,12},{6,14},{8,0},{10,2},{12,4},{14,6},{16,24},{18,... | collective-permute-start | bytes 786440 | tf_op jit(solution)/shard_map/ppermute | solution.py:28
  185.4 16.6 %collective-permute-start.3 = (bf16[8,8,4096]{2,1,0:T(8,128)(2,1)S(1)}, bf16[8,8,4096]{2,1,0:T(8,128)(2,1)S(1)}, u32[]{:S(2)}, u32[]{:S(2)}) collective-permute-start(bf16[8,8,4096]{2,1,0:T(8,128)(2,1)S(1)} %bitcast.65), channel_id=1, source_target_pairs={{0,16},{2,18},{4,20},{6,22},{8,24},{10,26},{12,28},{14,30},{16,0},... | collective-permute-start | bytes 1572872 | tf_op jit(solution)/shard_map/ppermute | solution.py:28
  205.9 118.8 %all-gather.6.cloned.1.call-start = ((), (), s32[]{:S(2)}) async-start(), calls=%async_computation.5 | async-start | bytes 2228224 | tf_op jit(solution)/shard_map/all_gather | solution.py:104
  267.8 127.0 %all-gather.8.cloned.1.call-start = ((), (), s32[]{:S(2)}) async-start(), calls=%async_computation.6 | async-start | bytes 2228224 | tf_op jit(solution)/shard_map/all_gather | solution.py:109
  324.7 5.4 %copy-start = (bf16[128,8192]{1,0:T(8,128)(2,1)S(1)}, bf16[128,8192]{1,0:T(8,128)(2,1)}, u32[]{:S(2)}) copy-start(bf16[128,8192]{1,0:T(8,128)(2,1)} %all-gather.6.cloned.1.call-done) | copy-start | bytes 6291460
  335.5 81.4 %copy-start.2 = (bf16[128,512]{1,0:T(8,128)(2,1)S(1)}, bf16[128,512]{1,0:T(8,128)(2,1)}, u32[]{:S(2)}) copy-start(bf16[128,512]{1,0:T(8,128)(2,1)} %all-reduce.3.cloned.1.call-done) | copy-start | bytes 393220
  335.6 81.4 %all-reduce.5.cloned.1.call-start = ((), (), s32[]{:S(2)}) async-start(), calls=%async_computation.7 | async-start | bytes 262144 | tf_op jit(solution)/shard_map/psum | solution.py:113
Sparse Core Ops, SparseCore 0:
  10.1 57.7 all-gather.3
  206.0 17.0 all-reduce.2
  267.9 56.7 all-gather.5
  335.7 59.0 all-gather.7
  400.9 16.0 all-reduce.4
